TPU v7x, 256 devices: a whole 4x4x8 slice. The times are simulated.
256 devices in a mesh: rep: 64 (over z, x, core), rows: 4 (over y).
Axes of the slice: x: 4, y: 4, z: 8, core: 2. Of those that a mesh axis runs over, the one named last changes fastest.
Arguments:
- pooled_grad: bfloat16 [262144, 2, 128], P(('rep', 'rows')), may hold values from -6 to 6
- slot_source: int32 [256, 4, 1024], P(('rep', 'rows')), may hold values from 0 to 2047, as said below
- slot_target: int32 [256, 4, 1024], P(('rep', 'rows')), may hold values from 0 to 8191, as said below
- slot_count: int32 [256, 4], P(('rep', 'rows')), may hold values from 128 to 1024, as said below
- table_rows: float32 [2, 16384, 128], P(None, 'rows'), may hold values from -1.5 to 1.5
- accum: float32 [2, 16384], P(None, 'rows'), may hold values from 0.01 to 1
Outputs:
- new_rows: float32 [2, 16384, 128], P(None, 'rows')
- new_accum: float32 [2, 16384], P(None, 'rows')
Inputs may be any that keep to these rules, and one draw needn't show every extreme that they name: `slot_source`: entry q encodes a local sample q // 2 and a table q % 2; the table agrees with that of slot_target at the same slot. `slot_target`: entry t encodes a table t // 4096 and a row t % 4096 of the owner's shard; rows repeat across slots and senders. `slot_count`: slots at or past the count carry no lookup; every sender fills all slots to some owner.
All inputs are finite; a program needn't handle non-finite values.
Results may differ from a plain program's by a relative error of at most 0.0003.
Values may be sent and summed in bfloat16 or wider, within the bound.
No kernel may reach another device: no remote copies, remote signals or barrier semaphores. Data moves between devices by JAX's collectives and lax.ppermute only.
A program may use at most 64 MiB of HBM per device.

v0:
```python
import math

import jax
import jax.numpy as jnp
from jax import lax
from jax.sharding import Mesh
from jax.sharding import PartitionSpec as P

REP_ROWS = ("rep_0", "rep_1", "rep_2", "rows")


LEARN_RATE = 0.1
EPSILON = 1e-06


def rows_for(lines, count):
    spare = -len(lines) % count
    return jnp.pad(lines, [(0, spare)] + [(0, 0)] * (lines.ndim - 1))


def copy_for_each(shard, axis):
    count = lax.axis_size(axis)
    return lax.all_to_all(
        jnp.broadcast_to(shard[None], (count, *shard.shape)), axis, 0, 0, tiled=True
    )


def in_order(parts, dim):
    shape = list(parts.shape[1:])
    shape[dim] *= parts.shape[0]
    return jnp.moveaxis(parts, 0, dim).reshape(shape)


def gather_axes(shard, axes, dim):
    far, near = axes
    leading = copy_for_each(shard, far)
    parts = jnp.swapaxes(copy_for_each(leading, near), 0, 1)
    return in_order(parts.reshape(-1, *shard.shape), dim)


def in_blocks(shard, dim, count):
    shape = shard.shape
    parts = shard.reshape(*shape[:dim], count, shape[dim] // count, *shape[dim + 1 :])
    return jnp.moveaxis(parts, dim, 0)


def summed_on_arrival(shard, axis, dim):
    count = lax.axis_size(axis)
    parts = lax.all_to_all(in_blocks(shard, dim, count), axis, 0, 0, tiled=True)
    return jnp.sum(parts, axis=0)


def sum_by_axis(shard, axes, dim):
    far, near = axes
    own = summed_on_arrival(in_blocks(shard, dim, lax.axis_size(far)), near, dim + 1)
    return jnp.sum(lax.all_to_all(own, far, 0, 0, tiled=True), axis=0)


def nested_sum(shard, axes):
    lines = shard.reshape(-1, shard.shape[-1])
    padded = rows_for(lines, lax.axis_size(axes[0]) * lax.axis_size(axes[1]))
    whole = gather_axes(sum_by_axis(padded, axes, 0), axes, 0)
    return lax.slice_in_dim(whole, 0, len(lines)).reshape(shard.shape)


def accumulate(grads, targets, tables, rows_dev):
    feature = grads.shape[-1]
    flat_rows = grads.reshape(-1, feature)
    lookup_keys = targets.reshape(-1)
    row_total = tables * rows_dev
    block_size = math.gcd(row_total, 512)
    block_count = row_total // block_size
    offsets = jnp.arange(block_size, dtype=jnp.int32)

    def row_block(block_index):
        row_base = block_index * block_size
        matches = (lookup_keys[:, None] == row_base + offsets[None, :]).astype(jnp.bfloat16)
        return jnp.einsum("sr,sw->rw", matches, flat_rows, preferred_element_type=jnp.float32)

    blocks = lax.map(row_block, jnp.arange(block_count, dtype=jnp.int32))
    return blocks.reshape(tables, rows_dev, feature)


def pick_rows(flat_grad, lookup_keys):
    slot_total = lookup_keys.shape[0]
    block_size = math.gcd(slot_total, 1024)
    block_count = slot_total // block_size
    sources = jnp.arange(flat_grad.shape[0], dtype=jnp.int32)
    key_blocks = lookup_keys.reshape(block_count, block_size)

    def slot_block(block_keys):
        matches = (block_keys[:, None] == sources[None, :]).astype(jnp.bfloat16)
        return jnp.dot(matches, flat_grad, preferred_element_type=jnp.float32).astype(jnp.bfloat16)

    blocks = lax.map(slot_block, key_blocks)
    return blocks.reshape(slot_total, flat_grad.shape[1])


def adagrad(rows_part, state_part, row_grad):
    updated = state_part + jnp.mean(row_grad * row_grad, axis=2)
    shifted = rows_part - LEARN_RATE * row_grad / (jnp.sqrt(updated)[:, :, None] + EPSILON)
    return (shifted, updated)


def shards(pooled_grad, slot_source, slot_target, slot_count, table_rows, accum):
    tables = pooled_grad.shape[1]
    feature = pooled_grad.shape[2]
    rows_dev = table_rows.shape[1]
    owner_total = slot_source.shape[1]
    slot_total = slot_source.shape[2]
    flat_grad = pooled_grad.reshape(-1, feature)
    source = slot_source[0]
    target = slot_target[0]
    counts = slot_count[0]
    slot_ids = jnp.arange(slot_total, dtype=jnp.int32)
    filled = slot_ids[None, :] < counts[:, None]
    source_keys = jnp.where(filled, source, -1).reshape(-1)
    picked = pick_rows(flat_grad, source_keys).reshape(owner_total, slot_total, feature)
    targets = jnp.where(filled, target, -1)
    got_grads, got_targets = (
        lax.all_to_all(picked, "rows", split_axis=0, concat_axis=0, tiled=True),
        lax.all_to_all(targets, "rows", split_axis=0, concat_axis=0, tiled=True),
    )
    partial_grad = accumulate(got_grads, got_targets, tables, rows_dev)
    row_grad = nested_sum(partial_grad, (("rep_0", "rep_1"), "rep_2"))
    new_rows, new_accum = adagrad(table_rows, accum, row_grad)
    return (new_rows, new_accum)


def solution(mesh):
    split = Mesh(
        mesh.devices.reshape(8, 4, 2, mesh.shape["rows"]), ("rep_0", "rep_1", "rep_2", "rows")
    )
    placed = (
        P(REP_ROWS, None, None),
        P(REP_ROWS, None, None),
        P(REP_ROWS, None, None),
        P(REP_ROWS, None),
        P(None, "rows", None),
        P(None, "rows"),
    )
    return jax.shard_map(
        shards,
        mesh=split,
        in_specs=placed,
        out_specs=(P(None, "rows", None), P(None, "rows")),
        check_vma=False,
    )
```

profile of v0, /device:TPU:1, one launch (start us, length us, event | category | flops | bytes accessed | tf_op | source)
XLA Modules:
  0.0 269.6 jit_solution(3844847864048092937)
XLA Ops:
  0.6 1.4 compare_select_fusion
  2.0 5.0 %all-to-all-start = ((s32[4,1,1024]{2,1,0:T(1,128)}), s32[4,1,1024]{2,1,0:T(1,128)S(1)}, u32[]{:S(2)}, u32[]{:S(2)}) async-start(s32[4,1,1024]{2,1,0:T(1,128)} %compare_select_fusion), calls=%async_computation | async-start | bytes 32768 | tf_op jit(solution)/shard_map/all_to_all | solution.py:122
  7.0 0.8 bitcast_select_fusion
  7.8 12.9 %while.22 = (s32[]{:T(128)}, bf16[4,1024,128]{2,1,0:T(8,128)(2,1)}, s32[4,1024]{1,0:T(4,128)S(1)}, bf16[2048,128]{1,0:T(8,128)(2,1)}, s32[]{:T(128)}) while((s32[]{:T(128)}, bf16[4,1024,128]{2,1,0:T(8,128)(2,1)}, s32[4,1024]{1,0:T(4,128)S(1)}, bf16[2048,128]{1,0:T(8,128)(2,1)}, s32[]{:T(128)}) %tuple.50), condition=%wide.region_1.2_spmd.clone, body=%wide.region_0.1_spmd.clone.sunk | while | flops 539099136 | bytes 799297 | solution.py:95
  7.8 3.2 %fusion.27 = bf16[4,1024,128]{2,1,0:T(8,128)(2,1)} fusion(bf16[4,1024,128]{2,1,0:T(8,128)(2,1)} %get-tuple-element.167, s32[]{:T(128)} %get-tuple-element.166, bf16[2048,128]{1,0:T(8,128)(2,1)} %get-tuple-element.174, s32[1024]{0:T(1024)S(1)} %bitcast.54), kind=kOutput, calls=%fused_computation.7.clone.1 | convolution fusion | flops 539099136 | bytes 791040 | tf_op jit(solution)/shard_map/while/body/eval_jaxpr/dot_general | solution.py:93
  11.1 3.2 %fusion.27 = bf16[4,1024,128]{2,1,0:T(8,128)(2,1)} fusion(bf16[4,1024,128]{2,1,0:T(8,128)(2,1)} %get-tuple-element.167, s32[]{:T(128)} %get-tuple-element.166, bf16[2048,128]{1,0:T(8,128)(2,1)} %get-tuple-element.174, s32[1024]{0:T(1024)S(1)} %bitcast.54), kind=kOutput, calls=%fused_computation.7.clone.1 | convolution fusion | flops 539099136 | bytes 791040 | tf_op jit(solution)/shard_map/while/body/eval_jaxpr/dot_general | solution.py:93
  14.3 3.2 %fusion.27 = bf16[4,1024,128]{2,1,0:T(8,128)(2,1)} fusion(bf16[4,1024,128]{2,1,0:T(8,128)(2,1)} %get-tuple-element.167, s32[]{:T(128)} %get-tuple-element.166, bf16[2048,128]{1,0:T(8,128)(2,1)} %get-tuple-element.174, s32[1024]{0:T(1024)S(1)} %bitcast.54), kind=kOutput, calls=%fused_computation.7.clone.1 | convolution fusion | flops 539099136 | bytes 791040 | tf_op jit(solution)/shard_map/while/body/eval_jaxpr/dot_general | solution.py:93
  17.5 3.2 %fusion.27 = bf16[4,1024,128]{2,1,0:T(8,128)(2,1)} fusion(bf16[4,1024,128]{2,1,0:T(8,128)(2,1)} %get-tuple-element.167, s32[]{:T(128)} %get-tuple-element.166, bf16[2048,128]{1,0:T(8,128)(2,1)} %get-tuple-element.174, s32[1024]{0:T(1024)S(1)} %bitcast.54), kind=kOutput, calls=%fused_computation.7.clone.1 | convolution fusion | flops 539099136 | bytes 791040 | tf_op jit(solution)/shard_map/while/body/eval_jaxpr/dot_general | solution.py:93
  20.7 4.2 %all-to-all-start.1 = ((bf16[4,1024,128]{2,1,0:T(8,128)(2,1)}), bf16[4,1024,128]{2,1,0:T(8,128)(2,1)S(1)}, u32[]{:S(2)}, u32[]{:S(2)}) async-start(bf16[4,1024,128]{2,1,0:T(8,128)(2,1)} %get-tuple-element.61), calls=%async_computation.1 | async-start | bytes 2097152 | tf_op jit(solution)/shard_map/all_to_all | solution.py:121
  25.0 13.2 %all-to-all-done.1 = bf16[4,1024,128]{2,1,0:T(8,128)(2,1)S(1)} async-done(((bf16[4,1024,128]{2,1,0:T(8,128)(2,1)}), bf16[4,1024,128]{2,1,0:T(8,128)(2,1)S(1)}, u32[]{:S(2)}, u32[]{:S(2)}) %all-to-all-start.1) | async-done | bytes 1048608 | tf_op jit(solution)/shard_map/all_to_all | solution.py:121
  38.2 78.5 %while.23 = (s32[]{:T(128)}, f32[16,512,128]{2,1,0:T(8,128)}, s32[4,1024]{1,0:T(4,128)S(1)}, s32[16]{0:T(128)S(1)}, bf16[4096,128]{1,0:T(8,128)(2,1)S(1)}, /*index=5*/s32[]{:T(128)}, s32[1]{0:T(128)}) while((s32[]{:T(128)}, f32[16,512,128]{2,1,0:T(8,128)}, s32[4,1024]{1,0:T(4,128)S(1)}, s32[16]{0:T(128)S(1)}, ...), condition=%wide.region_3.4_spmd.clone, body=%wide.region_2.3_spmd.clone.sunk | while | flops 538968576 | bytes 1364585 | solution.py:80
  38.2 0.6 dynamic_slice.14
  39.4 3.7 %fusion.30 = f32[16,512,128]{2,1,0:T(8,128)} fusion(f32[16,512,128]{2,1,0:T(8,128)} %get-tuple-element.184, s32[]{:T(128)} %get-tuple-element.183, bf16[4096,128]{1,0:T(8,128)(2,1)S(1)} %get-tuple-element.194, s32[512]{0:T(512)S(1)} %iota_add_fusion.2, s32[4096]{0:T(1024)S(1)} %bitcast.53), kind=kOutput, calls=%fused_computation.14.clone.1 | convolution fusion | flops 538968064 | bytes 1329664 | tf_op jit(solution)/shard_map/while/body/eval_jaxpr/sr,sw->rw/dot_general | solution.py:78
  43.1 0.6 dynamic_slice.14
  44.3 3.7 %fusion.30 = f32[16,512,128]{2,1,0:T(8,128)} fusion(f32[16,512,128]{2,1,0:T(8,128)} %get-tuple-element.184, s32[]{:T(128)} %get-tuple-element.183, bf16[4096,128]{1,0:T(8,128)(2,1)S(1)} %get-tuple-element.194, s32[512]{0:T(512)S(1)} %iota_add_fusion.2, s32[4096]{0:T(1024)S(1)} %bitcast.53), kind=kOutput, calls=%fused_computation.14.clone.1 | convolution fusion | flops 538968064 | bytes 1329664 | tf_op jit(solution)/shard_map/while/body/eval_jaxpr/sr,sw->rw/dot_general | solution.py:78
  48.0 0.6 dynamic_slice.14
  49.3 3.7 %fusion.30 = f32[16,512,128]{2,1,0:T(8,128)} fusion(f32[16,512,128]{2,1,0:T(8,128)} %get-tuple-element.184, s32[]{:T(128)} %get-tuple-element.183, bf16[4096,128]{1,0:T(8,128)(2,1)S(1)} %get-tuple-element.194, s32[512]{0:T(512)S(1)} %iota_add_fusion.2, s32[4096]{0:T(1024)S(1)} %bitcast.53), kind=kOutput, calls=%fused_computation.14.clone.1 | convolution fusion | flops 538968064 | bytes 1329664 | tf_op jit(solution)/shard_map/while/body/eval_jaxpr/sr,sw->rw/dot_general | solution.py:78
  52.9 0.6 dynamic_slice.14
  54.2 3.7 %fusion.30 = f32[16,512,128]{2,1,0:T(8,128)} fusion(f32[16,512,128]{2,1,0:T(8,128)} %get-tuple-element.184, s32[]{:T(128)} %get-tuple-element.183, bf16[4096,128]{1,0:T(8,128)(2,1)S(1)} %get-tuple-element.194, s32[512]{0:T(512)S(1)} %iota_add_fusion.2, s32[4096]{0:T(1024)S(1)} %bitcast.53), kind=kOutput, calls=%fused_computation.14.clone.1 | convolution fusion | flops 538968064 | bytes 1329664 | tf_op jit(solution)/shard_map/while/body/eval_jaxpr/sr,sw->rw/dot_general | solution.py:78
  57.8 0.6 dynamic_slice.14
  59.1 3.7 %fusion.30 = f32[16,512,128]{2,1,0:T(8,128)} fusion(f32[16,512,128]{2,1,0:T(8,128)} %get-tuple-element.184, s32[]{:T(128)} %get-tuple-element.183, bf16[4096,128]{1,0:T(8,128)(2,1)S(1)} %get-tuple-element.194, s32[512]{0:T(512)S(1)} %iota_add_fusion.2, s32[4096]{0:T(1024)S(1)} %bitcast.53), kind=kOutput, calls=%fused_computation.14.clone.1 | convolution fusion | flops 538968064 | bytes 1329664 | tf_op jit(solution)/shard_map/while/body/eval_jaxpr/sr,sw->rw/dot_general | solution.py:78
  62.7 0.6 dynamic_slice.14
  64.0 3.7 %fusion.30 = f32[16,512,128]{2,1,0:T(8,128)} fusion(f32[16,512,128]{2,1,0:T(8,128)} %get-tuple-element.184, s32[]{:T(128)} %get-tuple-element.183, bf16[4096,128]{1,0:T(8,128)(2,1)S(1)} %get-tuple-element.194, s32[512]{0:T(512)S(1)} %iota_add_fusion.2, s32[4096]{0:T(1024)S(1)} %bitcast.53), kind=kOutput, calls=%fused_computation.14.clone.1 | convolution fusion | flops 538968064 | bytes 1329664 | tf_op jit(solution)/shard_map/while/body/eval_jaxpr/sr,sw->rw/dot_general | solution.py:78
  67.6 0.6 dynamic_slice.14
  68.9 3.7 %fusion.30 = f32[16,512,128]{2,1,0:T(8,128)} fusion(f32[16,512,128]{2,1,0:T(8,128)} %get-tuple-element.184, s32[]{:T(128)} %get-tuple-element.183, bf16[4096,128]{1,0:T(8,128)(2,1)S(1)} %get-tuple-element.194, s32[512]{0:T(512)S(1)} %iota_add_fusion.2, s32[4096]{0:T(1024)S(1)} %bitcast.53), kind=kOutput, calls=%fused_computation.14.clone.1 | convolution fusion | flops 538968064 | bytes 1329664 | tf_op jit(solution)/shard_map/while/body/eval_jaxpr/sr,sw->rw/dot_general | solution.py:78
  73.8 3.7 %fusion.30 = f32[16,512,128]{2,1,0:T(8,128)} fusion(f32[16,512,128]{2,1,0:T(8,128)} %get-tuple-element.184, s32[]{:T(128)} %get-tuple-element.183, bf16[4096,128]{1,0:T(8,128)(2,1)S(1)} %get-tuple-element.194, s32[512]{0:T(512)S(1)} %iota_add_fusion.2, s32[4096]{0:T(1024)S(1)} %bitcast.53), kind=kOutput, calls=%fused_computation.14.clone.1 | convolution fusion | flops 538968064 | bytes 1329664 | tf_op jit(solution)/shard_map/while/body/eval_jaxpr/sr,sw->rw/dot_general | solution.py:78
  78.7 3.7 %fusion.30 = f32[16,512,128]{2,1,0:T(8,128)} fusion(f32[16,512,128]{2,1,0:T(8,128)} %get-tuple-element.184, s32[]{:T(128)} %get-tuple-element.183, bf16[4096,128]{1,0:T(8,128)(2,1)S(1)} %get-tuple-element.194, s32[512]{0:T(512)S(1)} %iota_add_fusion.2, s32[4096]{0:T(1024)S(1)} %bitcast.53), kind=kOutput, calls=%fused_computation.14.clone.1 | convolution fusion | flops 538968064 | bytes 1329664 | tf_op jit(solution)/shard_map/while/body/eval_jaxpr/sr,sw->rw/dot_general | solution.py:78
  82.4 0.6 dynamic_slice.14
  83.6 3.7 %fusion.30 = f32[16,512,128]{2,1,0:T(8,128)} fusion(f32[16,512,128]{2,1,0:T(8,128)} %get-tuple-element.184, s32[]{:T(128)} %get-tuple-element.183, bf16[4096,128]{1,0:T(8,128)(2,1)S(1)} %get-tuple-element.194, s32[512]{0:T(512)S(1)} %iota_add_fusion.2, s32[4096]{0:T(1024)S(1)} %bitcast.53), kind=kOutput, calls=%fused_computation.14.clone.1 | convolution fusion | flops 538968064 | bytes 1329664 | tf_op jit(solution)/shard_map/while/body/eval_jaxpr/sr,sw->rw/dot_general | solution.py:78
  88.5 3.7 %fusion.30 = f32[16,512,128]{2,1,0:T(8,128)} fusion(f32[16,512,128]{2,1,0:T(8,128)} %get-tuple-element.184, s32[]{:T(128)} %get-tuple-element.183, bf16[4096,128]{1,0:T(8,128)(2,1)S(1)} %get-tuple-element.194, s32[512]{0:T(512)S(1)} %iota_add_fusion.2, s32[4096]{0:T(1024)S(1)} %bitcast.53), kind=kOutput, calls=%fused_computation.14.clone.1 | convolution fusion | flops 538968064 | bytes 1329664 | tf_op jit(solution)/shard_map/while/body/eval_jaxpr/sr,sw->rw/dot_general | solution.py:78
  93.4 3.7 %fusion.30 = f32[16,512,128]{2,1,0:T(8,128)} fusion(f32[16,512,128]{2,1,0:T(8,128)} %get-tuple-element.184, s32[]{:T(128)} %get-tuple-element.183, bf16[4096,128]{1,0:T(8,128)(2,1)S(1)} %get-tuple-element.194, s32[512]{0:T(512)S(1)} %iota_add_fusion.2, s32[4096]{0:T(1024)S(1)} %bitcast.53), kind=kOutput, calls=%fused_computation.14.clone.1 | convolution fusion | flops 538968064 | bytes 1329664 | tf_op jit(solution)/shard_map/while/body/eval_jaxpr/sr,sw->rw/dot_general | solution.py:78
  98.3 3.7 %fusion.30 = f32[16,512,128]{2,1,0:T(8,128)} fusion(f32[16,512,128]{2,1,0:T(8,128)} %get-tuple-element.184, s32[]{:T(128)} %get-tuple-element.183, bf16[4096,128]{1,0:T(8,128)(2,1)S(1)} %get-tuple-element.194, s32[512]{0:T(512)S(1)} %iota_add_fusion.2, s32[4096]{0:T(1024)S(1)} %bitcast.53), kind=kOutput, calls=%fused_computation.14.clone.1 | convolution fusion | flops 538968064 | bytes 1329664 | tf_op jit(solution)/shard_map/while/body/eval_jaxpr/sr,sw->rw/dot_general | solution.py:78
  103.2 3.7 %fusion.30 = f32[16,512,128]{2,1,0:T(8,128)} fusion(f32[16,512,128]{2,1,0:T(8,128)} %get-tuple-element.184, s32[]{:T(128)} %get-tuple-element.183, bf16[4096,128]{1,0:T(8,128)(2,1)S(1)} %get-tuple-element.194, s32[512]{0:T(512)S(1)} %iota_add_fusion.2, s32[4096]{0:T(1024)S(1)} %bitcast.53), kind=kOutput, calls=%fused_computation.14.clone.1 | convolution fusion | flops 538968064 | bytes 1329664 | tf_op jit(solution)/shard_map/while/body/eval_jaxpr/sr,sw->rw/dot_general | solution.py:78
  108.2 3.7 %fusion.30 = f32[16,512,128]{2,1,0:T(8,128)} fusion(f32[16,512,128]{2,1,0:T(8,128)} %get-tuple-element.184, s32[]{:T(128)} %get-tuple-element.183, bf16[4096,128]{1,0:T(8,128)(2,1)S(1)} %get-tuple-element.194, s32[512]{0:T(512)S(1)} %iota_add_fusion.2, s32[4096]{0:T(1024)S(1)} %bitcast.53), kind=kOutput, calls=%fused_computation.14.clone.1 | convolution fusion | flops 538968064 | bytes 1329664 | tf_op jit(solution)/shard_map/while/body/eval_jaxpr/sr,sw->rw/dot_general | solution.py:78
  113.1 3.7 %fusion.30 = f32[16,512,128]{2,1,0:T(8,128)} fusion(f32[16,512,128]{2,1,0:T(8,128)} %get-tuple-element.184, s32[]{:T(128)} %get-tuple-element.183, bf16[4096,128]{1,0:T(8,128)(2,1)S(1)} %get-tuple-element.194, s32[512]{0:T(512)S(1)} %iota_add_fusion.2, s32[4096]{0:T(1024)S(1)} %bitcast.53), kind=kOutput, calls=%fused_computation.14.clone.1 | convolution fusion | flops 538968064 | bytes 1329664 | tf_op jit(solution)/shard_map/while/body/eval_jaxpr/sr,sw->rw/dot_general | solution.py:78
  116.7 2.5 copy.15
  119.2 10.6 %all_to_all.34 = f32[2,32,128,128]{3,2,1,0:T(8,128)} all-to-all(f32[2,32,128,128]{3,2,1,0:T(8,128)S(1)} %copy.15), channel_id=1, replica_groups=mesh['rep_0'=8,'rep_1'=4,'rep_2'=2,'rows'=4] {'rep_2'}, dimensions={0} | all-to-all | bytes 8388608 | tf_op jit(solution)/shard_map/all_to_all | solution.py:49
  129.8 2.7 %reduce_sum.27 = f32[32,128,128]{2,1,0:T(8,128)S(1)} reduce(f32[2,32,128,128]{3,2,1,0:T(8,128)} %all_to_all.34, f32[]{:T(128)} %constant.22.clone.1), dimensions={0}, to_apply=%region_4.5 | reduce | flops 524288 | bytes 6291460 | tf_op jit(solution)/shard_map/reduce_sum | solution.py:50
  132.5 59.8 %all_to_all.35 = f32[32,128,128]{2,1,0:T(8,128)} all-to-all(f32[32,128,128]{2,1,0:T(8,128)S(1)} %reduce_sum.27), channel_id=1, replica_groups=mesh['rep_0'=8,'rep_1'=4,'rep_2'=2,'rows'=4] {'rep_0','rep_1'}, dimensions={0} | all-to-all | bytes 4194304 | tf_op jit(solution)/shard_map/all_to_all | solution.py:56
  192.3 1.7 reduce_sum.28
  194.2 54.1 %all_to_all.36 = f32[32,128,128]{2,1,0:T(8,128)S(1)} all-to-all(f32[32,128,128]{2,1,0:T(8,128)S(1)} %broadcast_in_dim.42), channel_id=1, replica_groups=mesh['rep_0'=8,'rep_1'=4,'rep_2'=2,'rows'=4] {'rep_0','rep_1'}, dimensions={0} | all-to-all | bytes 4194304 | tf_op jit(solution)/shard_map/all_to_all | solution.py:23
  248.9 10.2 %all_to_all.37 = f32[2,32,128,128]{3,2,1,0:T(8,128)S(1)} all-to-all(f32[2,32,128,128]{3,2,1,0:T(8,128)S(1)} %broadcast_in_dim.43), channel_id=1, replica_groups=mesh['rep_0'=8,'rep_1'=4,'rep_2'=2,'rows'=4] {'rep_2'}, dimensions={0} | all-to-all | bytes 8388608 | tf_op jit(solution)/shard_map/all_to_all | solution.py:23
  259.0 2.0 copy-done
  261.1 1.1 multiply_reduce_fusion
  262.3 0.7 sqrt_add_fusion
  263.0 2.8 %copy_multiply_fusion = f32[2,32,128,128]{3,2,0,1:T(8,128)S(1)} fusion(f32[2,32,128,128]{3,2,1,0:T(8,128)} %copy-done), kind=kLoop, calls=%fused_computation.17 | loop fusion | flops 1048576 | bytes 8388608 | tf_op jit(solution)/shard_map/mul | solution.py:101
  265.7 0.7 copy-done.1
  266.4 3.1 %divide_subtract_fusion = f32[2,4096,128]{2,1,0:T(8,128)} fusion(f32[2,4096,128]{2,1,0:T(8,128)S(1)} %copy-done.1, f32[2,4096,128]{2,1,0:T(8,128)S(1)} %bitcast.48, f32[2,4096]{1,0:T(2,128)S(1)} %get-tuple-element.103), kind=kLoop, calls=%fused_computation.18 | loop fusion | flops 2097152 | bytes 12615680 | tf_op jit(solution)/shard_map/sub | solution.py:101
  (58 shorter events, 5.6 us)
Async XLA Ops:
  2.0 18.7 %all-to-all-start = ((s32[4,1,1024]{2,1,0:T(1,128)}), s32[4,1,1024]{2,1,0:T(1,128)S(1)}, u32[]{:S(2)}, u32[]{:S(2)}) async-start(s32[4,1,1024]{2,1,0:T(1,128)} %compare_select_fusion), calls=%async_computation | async-start | bytes 32768 | tf_op jit(solution)/shard_map/all_to_all | solution.py:122
  20.7 17.4 %all-to-all-start.1 = ((bf16[4,1024,128]{2,1,0:T(8,128)(2,1)}), bf16[4,1024,128]{2,1,0:T(8,128)(2,1)S(1)}, u32[]{:S(2)}, u32[]{:S(2)}) async-start(bf16[4,1024,128]{2,1,0:T(8,128)(2,1)} %get-tuple-element.61), calls=%async_computation.1 | async-start | bytes 2097152 | tf_op jit(solution)/shard_map/all_to_all | solution.py:121
  259.0 2.0 copy-start
  261.1 1.3 copy-start.2
  263.0 3.4 %copy-start.1 = (f32[2,4096,128]{2,1,0:T(8,128)S(1)}, f32[2,4096,128]{2,1,0:T(8,128)}, u32[]{:S(2)}) copy-start(f32[2,4096,128]{2,1,0:T(8,128)} %param.14) | copy-start | bytes 12582916
where the time goes:
time: 270 us
  blocking collectives  135 us (50%)
  matrix products  71.3 us (26%)
  local copies, waits for them, and re-layouts  15.4 us (6%)
  other arithmetic  14.4 us (5%)
  waiting for transfers between devices  13.2 us (5%)
  loops' own time  10.7 us (4%)
  starting transfers between devices  9.24 us (3%)
    all_to_all x2, blocking collectives, copy_for_each(): lax.all_to_all(jnp.broadcast_to(shard[None], (count, *shard.shape)), axis...  64.3 us
    all_to_all x1, blocking collectives, sum_by_axis(): return jnp.sum(lax.all_to_all(own, far, 0, 0, tiled=True), axis=0)  59.8 us
    dot_general x16, matrix products, row_block(): jnp.einsum('sr,sw->rw', matches, flat_rows, preferred_element_type=jnp.fl...  58.4 us
    all_to_all x1, waiting for transfers between devices, shards(): lax.all_to_all(picked, 'rows', split_axis=0, concat_axis=0, tiled=True)  13.2 us
    dot_general x4, matrix products, slot_block(): jnp.dot(matches, flat_grad, preferred_element_type=jnp.float32)  12.9 us
    another operation x1, loops' own time, accumulate(): blocks = lax.map(row_block, jnp.arange(block_count, dtype=jnp.int32))  10.7 us
    all_to_all x1, blocking collectives, summed_on_arrival(): parts = lax.all_to_all(in_blocks(shard, dim, count), axis, 0, 0, tiled=True)  10.6 us
    dynamic_slice x16, local copies, waits for them, and re-layouts, accumulate(): blocks = lax.map(row_block, jnp.arange(block_count, dtype=jnp.int32))  9.32 us
  transfers between devices with their start and end apart: 2, of which 1 were waited for; matrix products, arithmetic and copies ran while one was open for 5% of the time, Pallas kernels for 0%

commit v1 on v0

v1 whole, which is shorter than its diff:
```python
import functools

import jax
import jax.numpy as jnp
from jax import lax
from jax.experimental import pallas as pl
from jax.experimental.pallas import tpu as pltpu
from jax.sharding import Mesh
from jax.sharding import PartitionSpec as P

REP_ROWS = ("rep_0", "rep_1", "rep_2", "rows")
PLANE = ("rep_0", "rep_1")

LEARN_RATE = 0.1
EPSILON = 1e-06
LANES = 128
SPARE = 8
STEPS = 64.0
TOP = 32700.0
TINY = 1e-30

VM = pl.BlockSpec(memory_space=pltpu.VMEM)
SM = pl.BlockSpec(memory_space=pltpu.SMEM)


def pick_kernel(unroll, keys, flat, out, wide, stage):
    owners, cap, _ = out.shape
    wide[...] = flat[...].astype(jnp.float32)
    for owner in range(owners):
        slot = owner % 2

        def body(step, carry):
            first = step * unroll
            for u in range(unroll):
                key = keys[owner * cap + first + u]
                stage[slot, pl.ds(first + u, 1), :] = wide[pl.ds(key, 1), :]
            return carry

        lax.fori_loop(0, cap // unroll, body, 0)
        out[owner] = stage[slot].astype(jnp.bfloat16)


def pick_rows(keys, flat, owners):
    cap = keys.shape[0] // owners
    width = flat.shape[1]
    return pl.pallas_call(
        functools.partial(pick_kernel, 32),
        out_shape=jax.ShapeDtypeStruct((owners, cap, width), jnp.bfloat16),
        in_specs=[SM, VM],
        out_specs=VM,
        scratch_shapes=[
            pltpu.VMEM(flat.shape, jnp.float32),
            pltpu.VMEM((2, cap, width), jnp.float32),
        ],
        cost_estimate=pl.CostEstimate(flops=10**8, bytes_accessed=2 * 10**6, transcendentals=0),
        name="pick",
    )(keys, flat)


def scatter_kernel(unroll, core, keys, grads, mine, other, *scratch):
    senders, cap, _ = grads.shape
    sums, wides = scratch[:senders], scratch[senders:]
    half = mine.shape[0]
    for k in range(senders):
        wides[k][...] = grads[k].astype(jnp.float32)
        sums[k][...] = jnp.zeros(sums[k].shape, jnp.float32)

    def body(step, carry):
        first = step * unroll
        for u in range(unroll):
            for k in range(senders):
                key = keys[k * cap + first + u]
                sums[k][pl.ds(key, 1), :] += wides[k][pl.ds(first + u, 1), :]
        return carry

    lax.fori_loop(0, cap // unroll, body, 0)
    for out, index in ((mine, core[0]), (other, 1 - core[0])):
        base = pl.multiple_of(index * half, half)
        total = sums[0][pl.ds(base, half), :]
        for part in sums[1:]:
            total = total + part[pl.ds(base, half), :]
        out[...] = total


def scatter_add(core, keys, grads, rows):
    senders, cap, width = grads.shape
    shape = jax.ShapeDtypeStruct((rows // 2, width), jnp.float32)
    return pl.pallas_call(
        functools.partial(scatter_kernel, 4),
        out_shape=(shape, shape),
        in_specs=[SM, SM, VM],
        out_specs=(VM, VM),
        scratch_shapes=[pltpu.VMEM((rows + SPARE, width), jnp.float32)] * senders
        + [pltpu.VMEM((cap, width), jnp.float32)] * senders,
        compiler_params=pltpu.CompilerParams(vmem_limit_bytes=60 * 2**20),
        cost_estimate=pl.CostEstimate(flops=10**8, bytes_accessed=5 * 10**6, transcendentals=0),
        name="scatter",
    )(core, keys, grads)


def diagonal():
    shape = (LANES, LANES)
    return lax.broadcasted_iota(jnp.int32, shape, 0) == lax.broadcasted_iota(jnp.int32, shape, 1)


def to_row(column, diag):
    return jnp.sum(jnp.where(diag, column, 0.0), axis=0, keepdims=True)


def to_column(row, diag):
    return jnp.sum(jnp.where(diag, row, 0.0), axis=1, keepdims=True)


def encode(block, diag):
    peak = to_row(jnp.max(jnp.abs(block), axis=1, keepdims=True), diag)
    power = jnp.ceil(STEPS * jnp.log2(jnp.maximum(peak, TINY) / TOP))
    shrink = to_column(jnp.exp2(power * (-1.0 / STEPS)), diag)
    code = jnp.round(block * shrink).astype(jnp.int32).astype(jnp.int16)
    tail = jnp.broadcast_to(power, (SPARE, LANES)).astype(jnp.int32).astype(jnp.int16)
    return code, tail


def scale_row(tail):
    return jnp.exp2(tail.astype(jnp.int32).astype(jnp.float32)[0:1] * (1.0 / STEPS))


def encode_kernel(mine, got, out):
    diag = diagonal()

    def body(b, carry):
        rows = pl.ds(pl.multiple_of(b * LANES, LANES), LANES)
        code, tail = encode(mine[rows, :] + got[rows, :], diag)
        out[b, 0:LANES, :] = code
        out[b, LANES : LANES + SPARE, :] = tail
        return carry

    lax.fori_loop(0, out.shape[0], body, 0)


def encode_sum(mine, got):
    blocks = mine.shape[0] // LANES
    return pl.pallas_call(
        encode_kernel,
        out_shape=jax.ShapeDtypeStruct((blocks, LANES + SPARE, LANES), jnp.int16),
        in_specs=[VM, VM],
        out_specs=VM,
        name="encode",
    )(mine, got)


def reduce_kernel(parts, out):
    diag = diagonal()

    def body(j, total):
        scale = to_column(scale_row(parts[j, LANES : LANES + SPARE, :]), diag)
        return total + parts[j, 0:LANES, :].astype(jnp.int32).astype(jnp.float32) * scale

    total = lax.fori_loop(0, parts.shape[0], body, jnp.zeros((LANES, LANES), jnp.float32))
    code, tail = encode(total, diag)
    out[0:LANES, :] = code
    out[LANES : LANES + SPARE, :] = tail


def reduce_parts(parts):
    return pl.pallas_call(
        reduce_kernel,
        out_shape=jax.ShapeDtypeStruct(parts.shape[1:], jnp.int16),
        in_specs=[VM],
        out_specs=VM,
        name="reduce",
    )(parts)


def update_kernel(blocks, core, mine, got, rows, state, new_rows, new_state):
    diag = diagonal()
    base = pl.program_id(0) * blocks
    for table in range(2):
        own = core[0] == table
        for k in range(blocks):
            pair = [ref[base + k].astype(jnp.int32) for ref in (mine, got)]
            data = jnp.where(own, pair[0], pair[1]).astype(jnp.float32)
            code = data[0:LANES]
            scale = jnp.exp2(data[LANES : LANES + 1] * (1.0 / STEPS))
            squares = to_row(jnp.sum(code * code, axis=1, keepdims=True), diag)
            lanes = pl.ds(k * LANES, LANES)
            updated = state[pl.ds(table, 1), lanes] + squares * (scale * scale) * (1.0 / LANES)
            new_state[pl.ds(table, 1), lanes] = updated
            factor = to_column(LEARN_RATE * scale / (jnp.sqrt(updated) + EPSILON), diag)
            new_rows[table, lanes, :] = rows[table, lanes, :] - code * factor


def update(core, mine, got, rows, state):
    tables, rows_dev, width = rows.shape
    blocks = 4
    size = blocks * LANES
    row_spec = pl.BlockSpec((tables, size, width), lambda i: (0, i, 0))
    state_spec = pl.BlockSpec((tables, size), lambda i: (0, i))
    return pl.pallas_call(
        functools.partial(update_kernel, blocks),
        grid=(rows_dev // size,),
        out_shape=(
            jax.ShapeDtypeStruct(rows.shape, jnp.float32),
            jax.ShapeDtypeStruct(state.shape, jnp.float32),
        ),
        in_specs=[SM, VM, VM, row_spec, state_spec],
        out_specs=(row_spec, state_spec),
        name="update",
    )(core, mine, got, rows, state)


def swap_cores(x):
    return lax.ppermute(x, "rep_2", [(0, 1), (1, 0)])


def shards(pooled_grad, slot_source, slot_target, slot_count, table_rows, accum):
    feature = pooled_grad.shape[2]
    tables, rows_dev, _ = table_rows.shape
    owners, cap = slot_source.shape[1:]
    row_total = tables * rows_dev
    core = lax.axis_index("rep_2").astype(jnp.int32).reshape(1)
    flat_grad = pooled_grad.reshape(-1, feature)
    filled = jnp.arange(cap, dtype=jnp.int32)[None, :] < slot_count[0][:, None]
    targets = jnp.where(filled, slot_target[0], row_total)
    got_targets = lax.all_to_all(targets, "rows", 0, 0, tiled=True)
    picked = pick_rows(slot_source[0].reshape(-1), flat_grad, owners)
    got_grads = lax.all_to_all(picked, "rows", 0, 0, tiled=True)
    mine, other = scatter_add(core, got_targets.reshape(-1), got_grads, row_total)
    coded = encode_sum(mine, swap_cores(other))
    own = reduce_parts(lax.all_to_all(coded, PLANE, 0, 0, tiled=True))
    spread = jnp.broadcast_to(own[None], coded.shape)
    whole = lax.all_to_all(spread, PLANE, 0, 0, tiled=True)
    return update(core, whole, swap_cores(whole), table_rows, accum)


def solution(mesh):
    split = Mesh(
        mesh.devices.reshape(8, 4, 2, mesh.shape["rows"]), ("rep_0", "rep_1", "rep_2", "rows")
    )
    placed = (
        P(REP_ROWS, None, None),
        P(REP_ROWS, None, None),
        P(REP_ROWS, None, None),
        P(REP_ROWS, None),
        P(None, "rows", None),
        P(None, "rows"),
    )
    return jax.shard_map(
        shards,
        mesh=split,
        in_specs=placed,
        out_specs=(P(None, "rows", None), P(None, "rows")),
        check_vma=False,
    )
```

time: 270 us -> 162 us (0.60)
  matrix products: 71.3 us -> 0 us
  blocking collectives: 135 us -> 75.3 us
  Pallas kernels: 0 us -> 43.4 us
  other arithmetic: 14.4 us -> 1.4 us
  loops' own time: 10.7 us -> 0 us
  local copies, waits for them, and re-layouts: 15.4 us -> 5.56 us
  waiting for transfers between devices: 13.2 us -> 19.6 us
  starting transfers between devices: 9.24 us -> 15 us
    dot_general x20 -> x0, matrix products: 71.3 us -> none  [the longest x16 58.4 us: row_block(): jnp.einsum('sr,sw->rw', matches, flat_rows, preferred_element_type=jnp.fl...]
    all_to_all x4 -> x2, blocking collectives: 135 us -> 75.3 us  [the longest x1 41.5 us: shards(): own = reduce_parts(lax.all_to_all(coded, PLANE, 0, 0, tiled=True))]
    pallas_call x0 -> x5, Pallas kernels: none -> 43.4 us  [the longest x1 13 us: scatter_add(): pl.pallas_call(functools.partial(scatter_kernel, 4), out_shape=(shape, sh...]
    another operation x2 -> x0, loops' own time: 10.7 us -> none  [the longest x1 10.7 us: accumulate(): blocks = lax.map(row_block, jnp.arange(block_count, dtype=jnp.int32))]
    dynamic_slice x20 -> x0, local copies, waits for them, and re-layouts: 9.35 us -> none  [the longest x16 9.32 us: accumulate(): blocks = lax.map(row_block, jnp.arange(block_count, dtype=jnp.int32))]
    ppermute x0 -> x2, waiting for transfers between devices: none -> 6.38 us  [swap_cores(): return lax.ppermute(x, 'rep_2', [(0, 1), (1, 0)])]
    ppermute x0 -> x2, starting transfers between devices: none -> 5.75 us  [swap_cores(): return lax.ppermute(x, 'rep_2', [(0, 1), (1, 0)])]
    reduce_sum x3 -> x0, other arithmetic: 5.56 us -> none  [the longest x1 2.71 us: summed_on_arrival(): return jnp.sum(parts, axis=0)]
  transfers between devices with their start and end apart: 2 -> 4, of which waited for: 1 -> 3; matrix products, arithmetic and copies ran while one was open for 5% -> 1% of each run, Pallas kernels for 0% -> 4%
where the time goes in v1:
time: 162 us; the launch traced here: 161 us
  blocking collectives  75.3 us (46%)
  Pallas kernels  43.4 us (27%)
  waiting for transfers between devices  19.6 us (12%)
  starting transfers between devices  15 us (9%)
  local copies, waits for them, and re-layouts  5.56 us (3%)
    all_to_all x1, blocking collectives, shards(): own = reduce_parts(lax.all_to_all(coded, PLANE, 0, 0, tiled=True))  41.5 us
    all_to_all x1, blocking collectives, shards(): whole = lax.all_to_all(spread, PLANE, 0, 0, tiled=True)  33.8 us
    all_to_all x1, waiting for transfers between devices, shards(): got_grads = lax.all_to_all(picked, 'rows', 0, 0, tiled=True)  13.2 us
    pallas_call x1, Pallas kernels, scatter_add(): pl.pallas_call(functools.partial(scatter_kernel, 4), out_shape=(shape, sh...  13 us
    pallas_call x1, Pallas kernels, encode_sum(): pl.pallas_call(encode_kernel, out_shape=jax.ShapeDtypeStruct((blocks, LAN...  10 us
    pallas_call x1, Pallas kernels, update(): pl.pallas_call(functools.partial(update_kernel, blocks), grid=(rows_dev /...  9.04 us
    ppermute x2, waiting for transfers between devices, swap_cores(): return lax.ppermute(x, 'rep_2', [(0, 1), (1, 0)])  6.38 us
    pallas_call x1, Pallas kernels, pick_rows(): pl.pallas_call(functools.partial(pick_kernel, 32), out_shape=jax.ShapeDty...  5.99 us
  transfers between devices with their start and end apart: 4, of which 3 were waited for; matrix products, arithmetic and copies ran while one was open for 1% of the time, Pallas kernels for 4%

profile of v1, /device:TPU:1, one launch (start us, length us, event | category | flops | bytes accessed | tf_op | source)
XLA Modules:
  0.0 160.9 jit_solution(2250632163077509372)
XLA Ops:
  0.6 1.4 compare_select_fusion
  2.0 5.0 %all-to-all-start = ((s32[4,1,1024]{2,1,0:T(1,128)}), s32[4,1,1024]{2,1,0:T(1,128)S(1)}, u32[]{:S(2)}, u32[]{:S(2)}) async-start(s32[4,1,1024]{2,1,0:T(1,128)} %compare_select_fusion), calls=%async_computation | async-start | bytes 32768 | tf_op jit(solution)/shard_map/all_to_all | solution.py:224
  7.0 1.3 copy.10
  8.4 6.0 %pick.1 = bf16[4,1024,128]{2,1,0:T(8,128)(2,1)} custom-call(s32[4096]{0:T(1024)} %bitcast.10, bf16[2048,128]{1,0:T(8,128)(2,1)} %bitcast.8), custom_call_target="tpu_custom_call" | custom-call | flops 100000000 | bytes 2000000 | tf_op jit(solution)/shard_map/pick/pallas_call | solution.py:46
  14.3 0.0 all-to-all-done
  14.3 0.0 copy-start.4
  14.3 4.2 %all-to-all-start.1 = ((bf16[4,1024,128]{2,1,0:T(8,128)(2,1)}), bf16[4,1024,128]{2,1,0:T(8,128)(2,1)S(1)}, u32[]{:S(2)}, u32[]{:S(2)}) async-start(bf16[4,1024,128]{2,1,0:T(8,128)(2,1)} %pick.1), calls=%async_computation.1 | async-start | bytes 2097152 | tf_op jit(solution)/shard_map/all_to_all | solution.py:226
  18.6 13.2 %all-to-all-done.1.grads = bf16[4,1024,128]{2,1,0:T(8,128)(2,1)S(1)} async-done(((bf16[4,1024,128]{2,1,0:T(8,128)(2,1)}), bf16[4,1024,128]{2,1,0:T(8,128)(2,1)S(1)}, u32[]{:S(2)}, u32[]{:S(2)}) %all-to-all-start.1) | async-done | bytes 1048608 | tf_op jit(solution)/shard_map/all_to_all | solution.py:226
  31.8 0.0 copy-start.1
  31.8 0.0 copy-done.4
  31.8 1.0 copy-done.1
  32.8 13.0 %scatter.1 = (f32[4096,128]{1,0:T(8,128)}, f32[4096,128]{1,0:T(8,128)}) custom-call(s32[1]{0:T(128)} %bitcast.core, s32[4096]{0:T(1024)} %bitcast.9, bf16[4,1024,128]{2,1,0:T(8,128)(2,1)} %copy-done.1), custom_call_target="tpu_custom_call" | custom-call | flops 100000000 | bytes 5000000 | tf_op jit(solution)/shard_map/scatter/pallas_call | solution.py:88
  45.7 2.9 %collective-permute-start = (f32[4096,128]{1,0:T(8,128)}, f32[4096,128]{1,0:T(8,128)S(1)}, u32[]{:S(2)}, u32[]{:S(2)}) collective-permute-start(f32[4096,128]{1,0:T(8,128)} %get-tuple-element.5), channel_id=1, source_target_pairs={{0,4},{4,0},{1,5},{5,1},{2,6},{6,2},{3,7},{7,3},{8,12},{12,8},{9,1... | collective-permute-start | bytes 6291464 | tf_op jit(solution)/shard_map/ppermute | solution.py:212
  48.7 4.0 %collective-permute-done.got = f32[4096,128]{1,0:T(8,128)S(1)} collective-permute-done((f32[4096,128]{1,0:T(8,128)}, f32[4096,128]{1,0:T(8,128)S(1)}, u32[]{:S(2)}, u32[]{:S(2)}) %collective-permute-start) | collective-permute-done | bytes 2097184 | tf_op jit(solution)/shard_map/ppermute | solution.py:212
  52.6 0.0 copy-start.2
  52.7 1.3 copy-done.2
  54.0 10.0 %encode.1 = s16[32,136,128]{2,1,0:T(8,128)(2,1)} custom-call(f32[4096,128]{1,0:T(8,128)} %get-tuple-element.4.mine, f32[4096,128]{1,0:T(8,128)} %copy-done.2), custom_call_target="tpu_custom_call" | custom-call | tf_op jit(solution)/shard_map/encode/pallas_call | solution.py:142
  64.0 41.5 %all_to_all.21.parts = s16[32,136,128]{2,1,0:T(8,128)(2,1)} all-to-all(s16[32,136,128]{2,1,0:T(8,128)(2,1)} %encode.1), channel_id=1, replica_groups=mesh['rep_0'=8,'rep_1'=4,'rep_2'=2,'rows'=4] {'rep_0','rep_1'}, dimensions={0} | all-to-all | bytes 2228224 | tf_op jit(solution)/shard_map/all_to_all | solution.py:229
  105.5 5.4 %reduce.1 = s16[136,128]{1,0:T(8,128)(2,1)} custom-call(s16[32,136,128]{2,1,0:T(8,128)(2,1)} %all_to_all.21.parts), custom_call_target="tpu_custom_call" | custom-call | tf_op jit(solution)/shard_map/reduce/pallas_call | solution.py:165
  110.9 0.9 broadcast_in_dim.12
  111.8 33.8 %all_to_all.22.mine = s16[32,136,128]{2,1,0:T(8,128)(2,1)S(1)} all-to-all(s16[32,136,128]{2,1,0:T(8,128)(2,1)S(1)} %broadcast_in_dim.12), channel_id=1, replica_groups=mesh['rep_0'=8,'rep_1'=4,'rep_2'=2,'rows'=4] {'rep_0','rep_1'}, dimensions={0} | all-to-all | bytes 2228224 | tf_op jit(solution)/shard_map/all_to_all | solution.py:231
  145.6 0.0 copy-start
  145.6 2.8 %collective-permute-start.1 = (s16[32,136,128]{2,1,0:T(8,128)(2,1)S(1)}, s16[32,136,128]{2,1,0:T(8,128)(2,1)S(1)}, u32[]{:S(2)}, u32[]{:S(2)}) collective-permute-start(s16[32,136,128]{2,1,0:T(8,128)(2,1)S(1)} %all_to_all.22.mine), channel_id=1, source_target_pairs={{0,4},{4,0},{1,5},{5,1},{2,6},{6,2},{3,7},{7,3},{8,12},{12,8},{9,1... | collective-permute-start | bytes 3342344 | tf_op jit(solution)/shard_map/ppermute | solution.py:212
  148.5 2.4 %collective-permute-done.1.got = s16[32,136,128]{2,1,0:T(8,128)(2,1)S(1)} collective-permute-done((s16[32,136,128]{2,1,0:T(8,128)(2,1)S(1)}, s16[32,136,128]{2,1,0:T(8,128)(2,1)S(1)}, u32[]{:S(2)}, u32[]{:S(2)}) %collective-permute-start.1) | collective-permute-done | bytes 1114144 | tf_op jit(solution)/shard_map/ppermute | solution.py:212
  150.8 0.0 copy-done
  150.8 0.0 copy-start.3
  150.8 1.0 copy-done.3
  151.9 9.0 %update.1 = (f32[2,4096,128]{2,1,0:T(8,128)}, f32[2,4096]{1,0:T(2,128)}) custom-call(s32[1]{0:T(128)} %bitcast.core, s16[32,136,128]{2,1,0:T(8,128)(2,1)} %copy-done, s16[32,136,128]{2,1,0:T(8,128)(2,1)} %copy-done.3, f32[2,4096,128]{2,1,0:T(8,128)} %rows.1, f32[2,4096]{1,0:T(2,128)} %state.1), custom_call_target="tpu_custom_call" | custom-call | tf_op jit(solution)/shard_map/update/pallas_call | solution.py:198
Async XLA Ops:
  2.0 12.3 %all-to-all-start = ((s32[4,1,1024]{2,1,0:T(1,128)}), s32[4,1,1024]{2,1,0:T(1,128)S(1)}, u32[]{:S(2)}, u32[]{:S(2)}) async-start(s32[4,1,1024]{2,1,0:T(1,128)} %compare_select_fusion), calls=%async_computation | async-start | bytes 32768 | tf_op jit(solution)/shard_map/all_to_all | solution.py:224
  14.3 17.5 %copy-start.4 = (s32[4,1,1024]{2,1,0:T(1,128)}, s32[4,1,1024]{2,1,0:T(1,128)S(1)}, u32[]{:S(2)}) copy-start(s32[4,1,1024]{2,1,0:T(1,128)S(1)} %all-to-all-done) | copy-start | bytes 49156
  14.3 17.4 %all-to-all-start.1 = ((bf16[4,1024,128]{2,1,0:T(8,128)(2,1)}), bf16[4,1024,128]{2,1,0:T(8,128)(2,1)S(1)}, u32[]{:S(2)}, u32[]{:S(2)}) async-start(bf16[4,1024,128]{2,1,0:T(8,128)(2,1)} %pick.1), calls=%async_computation.1 | async-start | bytes 2097152 | tf_op jit(solution)/shard_map/all_to_all | solution.py:226
  31.8 1.0 copy-start.1
  45.7 6.9 %collective-permute-start = (f32[4096,128]{1,0:T(8,128)}, f32[4096,128]{1,0:T(8,128)S(1)}, u32[]{:S(2)}, u32[]{:S(2)}) collective-permute-start(f32[4096,128]{1,0:T(8,128)} %get-tuple-element.5), channel_id=1, source_target_pairs={{0,4},{4,0},{1,5},{5,1},{2,6},{6,2},{3,7},{7,3},{8,12},{12,8},{9,1... | collective-permute-start | bytes 6291464 | tf_op jit(solution)/shard_map/ppermute | solution.py:212
  52.6 1.3 copy-start.2
  145.6 5.2 %copy-start = (s16[32,136,128]{2,1,0:T(8,128)(2,1)}, s16[32,136,128]{2,1,0:T(8,128)(2,1)S(1)}, u32[]{:S(2)}) copy-start(s16[32,136,128]{2,1,0:T(8,128)(2,1)S(1)} %all_to_all.22.mine) | copy-start | bytes 3342340
  145.6 5.2 %collective-permute-start.1 = (s16[32,136,128]{2,1,0:T(8,128)(2,1)S(1)}, s16[32,136,128]{2,1,0:T(8,128)(2,1)S(1)}, u32[]{:S(2)}, u32[]{:S(2)}) collective-permute-start(s16[32,136,128]{2,1,0:T(8,128)(2,1)S(1)} %all_to_all.22.mine), channel_id=1, source_target_pairs={{0,4},{4,0},{1,5},{5,1},{2,6},{6,2},{3,7},{7,3},{8,12},{12,8},{9,1... | collective-permute-start | bytes 3342344 | tf_op jit(solution)/shard_map/ppermute | solution.py:212
  150.8 1.0 copy-start.3
